TPU v7x, 256 devices: a 4x2x16 block of a 4x16x16 slice. The times are simulated.
256 devices in a mesh: rep: 2 (over y), ep: 128 (over x, z, core).
Axes of the slice: x: 4, y: 2, z: 16, core: 2. Of those that a mesh axis runs over, the one named last changes fastest.
The devices are a block of a 4x16x16 slice.
Arguments:
- cache_kv: bfloat16 [512, 2048, 576], P(('rep', 'ep')), parts along dimension 0, may hold values from -6 to 6
- new_kv: bfloat16 [512, 2, 576], P(('rep', 'ep')), parts along dimension 0, may hold values from -6 to 6
- queries: bfloat16 [512, 2, 64, 576], P(('rep', 'ep')), parts along dimension 0, may hold values from -256 to 256
- lengths: int32 [512], P(('rep', 'ep')), parts along dimension 0, may hold values from 256 to 2048
- resid: bfloat16 [512, 2, 7168], P(('rep', 'ep')), parts along dimension 0, may hold values from -18 to 18
- value_up: bfloat16 [512, 8192], P(None, 'ep'), may hold values from -1.5 to 1.5
- out_proj: bfloat16 [8192, 7168], P('ep'), may hold values from -0.09375 to 0.09375
- norm_gain: bfloat16 [7168], replicated, may hold values from 0.25 to 1.75
- router: bfloat16 [7168, 16], replicated, may hold values from -0.0625 to 0.0625
- expert_ids: int32 [512, 2, 8], P(('rep', 'ep')), parts along dimension 0, may hold values from 0 to 15, as said below
- slots: int32 [512, 2, 8], P(('rep', 'ep')), parts along dimension 0, may hold values from 0 to 3, as said below
- w_gate: bfloat16 [7168, 16384], P(None, 'ep'), may hold values from -0.0625 to 0.0625
- w_up: bfloat16 [7168, 16384], P(None, 'ep'), may hold values from -0.0625 to 0.0625
- w_down: bfloat16 [16384, 7168], P('ep'), may hold values from -0.1875 to 0.1875
Outputs:
- mixed: bfloat16 [512, 2, 7168], P(('rep', 'ep')), parts along dimension 0
There are 2 independent parts, one for each index of `rep`. A program takes and returns all parts, laid end to end along the dimension named above; an argument that names none is the same for every part. Nothing has to cross between parts.
Inputs may be any that keep to these rules, and one draw needn't show every extreme that they name: `expert_ids`: each row names 8 different experts. In each aligned block of 4 rows (the rows of one device), the rows that name the same expert carry the distinct slots 0 up to their number minus one for it; in every block some expert is named by all 4 rows.
All inputs are finite; a program needn't handle non-finite values.
Results may differ from a plain program's by a relative error of at most 0.0065.
Values may be sent and summed in bfloat16 or wider, within the bound.
No kernel may reach another device: no remote copies, remote signals or barrier semaphores. Data moves between devices by JAX's collectives and lax.ppermute only.
A program may use at most 128 MiB of HBM per device.

v0:
```python
import math
import jax
import jax.numpy as jnp
from jax import lax
from jax.sharding import PartitionSpec as P

D = 7168
H = 64
LAT = 512
VH = 128
EXPERTS = 16
TOP = 8
CAP = 2
QK = 192
route_scale = 2.827
norm_eps = 1e-06


def softmax_parts(score_cache, score_new):
    row_peak = jnp.maximum(jnp.max(score_cache, axis=-1), jnp.max(score_new, axis=-1))
    exp_cache = jnp.exp(score_cache - row_peak[..., None])
    exp_new = jnp.exp(score_new - row_peak[..., None])
    exp_total = jnp.sum(exp_cache, axis=-1) + jnp.sum(exp_new, axis=-1)
    prob_cache = (exp_cache / exp_total[..., None]).astype(jnp.bfloat16)
    prob_new = (exp_new / exp_total[..., None]).astype(jnp.bfloat16)
    return (prob_cache, prob_new)


def attention(cache_kv, new_kv, queries, lengths):
    score_scale = 1.0 / math.sqrt(QK)
    cache_len = cache_kv.shape[1]
    step_count = new_kv.shape[1]
    score_new = (
        jnp.einsum("bshk,btk->bsht", queries, new_kv, preferred_element_type=jnp.float32)
        * score_scale
    )
    step_ids = jnp.arange(step_count, dtype=jnp.int32)
    causal = step_ids[None, :] <= step_ids[:, None]
    score_new = jnp.where(causal[None, :, None, :], score_new, -jnp.inf)
    score_cache = (
        jnp.einsum("bshk,bpk->bshp", queries, cache_kv, preferred_element_type=jnp.float32)
        * score_scale
    )
    position = jnp.arange(cache_len, dtype=jnp.int32)
    is_live = position[None, :] < lengths[:, None]
    score_cache = jnp.where(is_live[:, None, None, :], score_cache, -jnp.inf)
    prob_cache, prob_new = softmax_parts(score_cache, score_new)
    context = jnp.einsum(
        "bshp,bpc->bshc", prob_cache, cache_kv[:, :, :LAT], preferred_element_type=jnp.float32
    )
    context = context + jnp.einsum(
        "bsht,btc->bshc", prob_new, new_kv[:, :, :LAT], preferred_element_type=jnp.float32
    )
    return context.astype(jnp.bfloat16)


def expert_ffn(token_rows, w_gate, w_up, w_down):
    gate = jnp.dot(token_rows, w_gate, preferred_element_type=jnp.float32)
    upward = jnp.dot(token_rows, w_up, preferred_element_type=jnp.float32)
    act = (jax.nn.silu(gate) * upward).astype(jnp.bfloat16)
    return jnp.dot(act, w_down, preferred_element_type=jnp.float32)


def route_weights(token_rows, route_ids, router):
    logits = jnp.dot(token_rows, router, preferred_element_type=jnp.float32)
    expert_range = jnp.arange(router.shape[1], dtype=jnp.int32)
    is_pick = route_ids[:, :, None] == expert_range[None, None, :]
    picked = jnp.sum(jnp.where(is_pick, logits[:, None, :], 0.0), axis=-1)
    gates = jax.nn.sigmoid(picked)
    return route_scale * gates / jnp.sum(gates, axis=1, keepdims=True)


def body(
    cache_kv,
    new_kv,
    queries,
    lengths,
    resid,
    value_up,
    out_proj,
    norm_gain,
    router,
    expert_ids,
    slots,
    w_gate,
    w_up,
    w_down,
):
    devices = lax.axis_size("ep")
    context = attention(cache_kv, new_kv, queries, lengths)
    tok_count = context.shape[0] * context.shape[1]
    context = context.reshape(tok_count, H, LAT)
    value_cols = value_up.shape[1]
    heads_per = max(1, value_cols // VH)
    outgoing = jnp.repeat(context, VH // value_cols, axis=1)
    arrived = lax.all_to_all(outgoing, "ep", split_axis=1, concat_axis=0, tiled=True)
    value_table = value_up.reshape(LAT, heads_per, value_cols // heads_per)
    values = jnp.einsum("rhc,chv->rhv", arrived, value_table, preferred_element_type=jnp.float32)
    values = values.astype(jnp.bfloat16).reshape(devices * tok_count, value_cols)
    turned = lax.all_to_all(out_proj, "ep", split_axis=1, concat_axis=0, tiled=True)
    column_share = jnp.dot(
        lax.all_gather(values, "ep", axis=1, tiled=True), turned, preferred_element_type=jnp.float32
    )
    attended = lax.all_to_all(column_share, "ep", split_axis=0, concat_axis=1, tiled=True)
    hidden = resid.reshape(tok_count, D).astype(jnp.float32) + attended
    mean_square = jnp.mean(hidden * hidden, axis=-1, keepdims=True)
    normed = (hidden * lax.rsqrt(mean_square + norm_eps) * norm_gain.astype(jnp.float32)).astype(
        jnp.bfloat16
    )
    route_ids = expert_ids.reshape(tok_count, TOP)
    route_slots = slots.reshape(tok_count, TOP)
    group_size = devices // EXPERTS
    weights = route_weights(normed, route_ids, router)
    expert_grid = (
        route_ids[:, :, None] == jnp.arange(EXPERTS, dtype=jnp.int32)[None, None, :]
    ).astype(jnp.float32)
    slot_grid = (route_slots[:, :, None] == jnp.arange(CAP, dtype=jnp.int32)[None, None, :]).astype(
        jnp.float32
    )
    places = jnp.sum(expert_grid[:, :, :, None] * slot_grid[:, :, None, :], axis=1)
    shares = jnp.sum(
        expert_grid[:, :, :, None] * slot_grid[:, :, None, :] * weights[:, :, None, None], axis=1
    )
    places_dest = jnp.repeat(places, group_size, axis=1)
    shares_dest = jnp.repeat(shares, group_size, axis=1)
    outgoing_rows = jnp.einsum(
        "tjc,td->jcd", places_dest.astype(jnp.bfloat16), normed, preferred_element_type=jnp.float32
    ).astype(jnp.bfloat16)
    slot_rows = lax.all_to_all(outgoing_rows, "ep", split_axis=0, concat_axis=0, tiled=True)
    flat_rows = slot_rows.reshape(-1, slot_rows.shape[2])
    produced = expert_ffn(flat_rows, w_gate, w_up, w_down)
    produced = produced.reshape(slot_rows.shape[0], slot_rows.shape[1], produced.shape[1])
    returned = lax.all_to_all(
        produced.astype(jnp.bfloat16), "ep", split_axis=0, concat_axis=0, tiled=True
    ).astype(produced.dtype)
    expert_mix = jnp.dot(
        shares_dest.reshape(tok_count, devices * CAP),
        returned.reshape(devices * CAP, D),
        precision=lax.Precision.HIGHEST,
    )
    mixed = (hidden + expert_mix).astype(jnp.bfloat16)
    return mixed.reshape(resid.shape)


def solution(mesh):
    return jax.shard_map(
        body,
        mesh=mesh,
        in_specs=(
            P(("rep", "ep"), None, None),
            P(("rep", "ep"), None, None),
            P(("rep", "ep"), None, None, None),
            P(("rep", "ep")),
            P(("rep", "ep"), None, None),
            P(None, "ep"),
            P("ep", None),
            P(),
            P(),
            P(("rep", "ep"), None, None),
            P(("rep", "ep"), None, None),
            P(None, "ep"),
            P(None, "ep"),
            P("ep", None),
        ),
        out_specs=P(("rep", "ep"), None, None),
        check_vma=False,
    )
```

profile of v0, /device:TPU:164, one launch (start us, length us, event | category | flops | bytes accessed | tf_op | source)
XLA Modules:
  0.0 692.0 jit_solution(3392303585385041434)
XLA Ops:
  6.6 0.9 iota_compare_fusion.1
  7.5 3.8 fusion.41
  12.0 1.7 fusion.5
  14.4 61.0 %all_to_all.60 = bf16[4,128,512]{2,0,1:T(4,128)(2,1)S(1)} all-to-all(bf16[4,128,512]{2,0,1:T(4,128)(2,1)S(1)} %bitcast.75), channel_id=1, replica_groups=mesh['rep'=2,'ep'=128] {'ep'}, dimensions={1} | all-to-all | bytes 1048576 | tf_op jit(solution)/shard_map/all_to_all | solution.py:96
  75.6 0.9 convolution_convert_fusion.2
  76.5 2.6 copy.54
  79.2 3.4 reshape.151
  82.6 62.4 %all_to_all.61 = bf16[128,2,1792]{2,1,0:T(2,128)(2,1)} all-to-all(bf16[128,2,1792]{2,1,0:T(2,128)(2,1)S(1)} %reshape.151), channel_id=1, replica_groups=mesh['rep'=2,'ep'=128] {'ep'}, dimensions={0} | all-to-all | bytes 1835008 | tf_op jit(solution)/shard_map/all_to_all | solution.py:100
  145.0 4.3 reshape.152
  149.3 1.6 bitcast_bitcast_fusion
  151.0 1.8 copy.43
  152.7 3.0 reshape.147
  155.7 61.1 %all-gather.2.cloned.1.call-done = bf16[512,8192]{0,1:T(8,128)(2,1)} async-done(((bf16[512,64]{0,1:T(8,128)(2,1)}), bf16[512,8192]{0,1:T(8,128)(2,1)}) %all-gather.2.cloned.1.call-update) | async-done | bytes 8388624 | tf_op jit(solution)/shard_map/all_gather | solution.py:102
  216.8 11.4 %copy.41 = bf16[512,8192]{1,0:T(8,128)(2,1)} copy(bf16[512,8192]{0,1:T(8,128)(2,1)} %all-gather.2.cloned.1.call-done) | data formatting | bytes 16777216 | tf_op jit(solution)/shard_map/all_gather | solution.py:102
  228.2 13.1 %dot_general.43 = bf16[128,4,8192]{2,1,0:T(4,128)(2,1)} reshape(bf16[512,8192]{1,0:T(8,128)(2,1)} %copy.41) | data formatting | bytes 16777216 | tf_op jit(solution)/shard_map/dot_general | solution.py:101
  241.3 12.4 %fusion = f32[128,4,56]{0,2,1:T(8,128)S(1)} fusion(bf16[8192,56,1]{0,1,2:T(8,128)(2,1)S(1)} %reshape.147, bf16[128,4,8192]{2,1,0:T(4,128)(2,1)} %dot_general.43), kind=kOutput, calls=%fused_computation.2 | convolution fusion | flops 469762048 | bytes 9420800 | tf_op jit(solution)/shard_map/dot_general | solution.py:101
  253.8 0.9 reshape.153
  254.8 14.2 %all-to-all-start.2 = ((f32[128,1,224]{2,1,0:T(1,128)}), f32[128,1,224]{2,1,0:T(1,128)S(1)}, u32[]{:S(2)}, u32[]{:S(2)}) async-start(f32[128,1,224]{2,1,0:T(1,128)} %reshape.153), calls=%async_computation.2 | async-start | bytes 262144 | tf_op jit(solution)/shard_map/all_to_all | solution.py:104
  269.5 14.2 %all-to-all-done.2 = f32[128,1,224]{2,1,0:T(1,128)S(1)} async-done(((f32[128,1,224]{2,1,0:T(1,128)}), f32[128,1,224]{2,1,0:T(1,128)S(1)}, u32[]{:S(2)}, u32[]{:S(2)}) %all-to-all-start.2) | async-done | bytes 114720 | tf_op jit(solution)/shard_map/all_to_all | solution.py:104
  284.2 1.0 reduce.1
  287.0 1.2 convolution_convert_fusion.1
  288.2 3.8 copy.49
  292.0 176.9 %all_to_all.62 = bf16[128,2,7168]{2,1,0:T(2,128)(2,1)} all-to-all(bf16[128,2,7168]{2,1,0:T(2,128)(2,1)S(1)} %copy.49), channel_id=1, replica_groups=mesh['rep'=2,'ep'=128] {'ep'}, dimensions={0} | all-to-all | bytes 7340032 | tf_op jit(solution)/shard_map/all_to_all | solution.py:129
  468.9 8.4 %reshape.138 = bf16[256,7168]{1,0:T(8,128)(2,1)} reshape(bf16[128,2,7168]{2,1,0:T(2,128)(2,1)} %all_to_all.62) | data formatting | bytes 7340032 | tf_op jit(solution)/shard_map/reshape | solution.py:130
  477.3 3.7 fusion.43
  481.0 6.6 convolution_convert_fusion
  487.6 8.1 %convert_element_type.95 = bf16[128,2,7168]{2,1,0:T(2,128)(2,1)} reshape(bf16[256,7168]{1,0:T(8,128)(2,1)} %convolution_convert_fusion) | data formatting | bytes 7340032 | tf_op jit(solution)/shard_map/convert_element_type | solution.py:134
  495.7 10.9 %all-to-all-start.4 = ((bf16[128,2,7168]{2,1,0:T(2,128)(2,1)}), bf16[128,2,7168]{2,1,0:T(2,128)(2,1)}, u32[]{:S(2)}, u32[]{:S(2)}) async-start(bf16[128,2,7168]{2,1,0:T(2,128)(2,1)} %convert_element_type.95), calls=%async_computation.4 | async-start | bytes 7340032 | tf_op jit(solution)/shard_map/all_to_all | solution.py:133
  506.8 165.5 %all-to-all-done.4 = bf16[128,2,7168]{2,1,0:T(2,128)(2,1)} async-done(((bf16[128,2,7168]{2,1,0:T(2,128)(2,1)}), bf16[128,2,7168]{2,1,0:T(2,128)(2,1)}, u32[]{:S(2)}, u32[]{:S(2)}) %all-to-all-start.4) | async-done | bytes 3670048 | tf_op jit(solution)/shard_map/all_to_all | solution.py:133
  672.3 8.4 %reshape.139 = bf16[256,7168]{1,0:T(8,128)(2,1)} reshape(bf16[128,2,7168]{2,1,0:T(2,128)(2,1)} %all-to-all-done.4) | data formatting | bytes 7340032 | tf_op jit(solution)/shard_map/reshape | solution.py:138
  680.7 3.6 fusion.2
  684.3 0.7 reshape.140
  (57 shorter events, 4.6 us)
Async XLA Ops:
  6.5 474.5 %copy-start = (bf16[128,7168]{1,0:T(8,128)(2,1)S(1)}, bf16[128,7168]{1,0:T(8,128)(2,1)}, u32[]{:S(2)}) copy-start(bf16[128,7168]{1,0:T(8,128)(2,1)} %param.27) | copy-start | bytes 5505028
  6.6 210.3 %all-gather.2.cloned.1.call-start = ((), (), s32[]{:S(2)}) async-start(), calls=%async_computation.5 | async-start | bytes 8454144 | tf_op jit(solution)/shard_map/all_gather | solution.py:102
  7.4 3.8 copy-start.2
  7.4 3.8 copy-start.8
  7.5 4.6 copy-start.1
  13.8 61.8 %copy-start.5 = (bf16[512,64]{0,1:T(8,128)(2,1)S(1)}, bf16[512,64]{0,1:T(8,128)(2,1)}, u32[]{:S(2)}) copy-start(bf16[512,64]{0,1:T(8,128)(2,1)} %param.19) | copy-start | bytes 196612
  241.3 27.7 %copy-start.4 = (bf16[2,2,7168]{2,1,0:T(2,128)(2,1)S(1)}, bf16[2,2,7168]{2,1,0:T(2,128)(2,1)}, u32[]{:S(2)}) copy-start(bf16[2,2,7168]{2,1,0:T(2,128)(2,1)} %param.18) | copy-start | bytes 172036
  241.3 28.0 %copy-start.6 = (bf16[7168]{0:T(1024)(128)(2,1)S(1)}, bf16[7168]{0:T(1024)(128)(2,1)}, u32[]{:S(2)}) copy-start(bf16[7168]{0:T(1024)(128)(2,1)} %param.21) | copy-start | bytes 43012
  241.3 28.1 %copy-start.9 = (s32[2,2,8]{2,1,0:T(2,128)S(1)}, s32[2,2,8]{2,1,0:T(2,128)}, u32[]{:S(2)}) copy-start(s32[2,2,8]{2,1,0:T(2,128)} %param.24) | copy-start | bytes 388
  241.3 28.1 %copy-start.7 = (s32[2,2,8]{2,1,0:T(2,128)S(1)}, s32[2,2,8]{2,1,0:T(2,128)}, u32[]{:S(2)}) copy-start(s32[2,2,8]{2,1,0:T(2,128)} %param.23) | copy-start | bytes 388
  253.7 32.1 %copy-start.3 = (bf16[7168,16]{0,1:T(8,128)(2,1)S(1)}, bf16[7168,16]{0,1:T(8,128)(2,1)}, u32[]{:S(2)}) copy-start(bf16[7168,16]{0,1:T(8,128)(2,1)} %param.22) | copy-start | bytes 688132
  254.8 28.9 %all-to-all-start.2 = ((f32[128,1,224]{2,1,0:T(1,128)}), f32[128,1,224]{2,1,0:T(1,128)S(1)}, u32[]{:S(2)}, u32[]{:S(2)}) async-start(f32[128,1,224]{2,1,0:T(1,128)} %reshape.153), calls=%async_computation.2 | async-start | bytes 262144 | tf_op jit(solution)/shard_map/all_to_all | solution.py:104
  495.7 176.5 %all-to-all-start.4 = ((bf16[128,2,7168]{2,1,0:T(2,128)(2,1)}), bf16[128,2,7168]{2,1,0:T(2,128)(2,1)}, u32[]{:S(2)}, u32[]{:S(2)}) async-start(bf16[128,2,7168]{2,1,0:T(2,128)(2,1)} %convert_element_type.95), calls=%async_computation.4 | async-start | bytes 7340032 | tf_op jit(solution)/shard_map/all_to_all | solution.py:133
Sparse Core Ops, SparseCore 0:
  76.7 140.1 all-gather.1
where the time goes:
time: 702 us; the launch traced here: 692 us
  blocking collectives  300 us (43%)
  waiting for transfers between devices  241 us (34%)
  local copies, waits for them, and re-layouts  73.9 us (11%)
  matrix products  34.7 us (5%)
  starting transfers between devices  25.1 us (4%)
  between operations  14 us (2%)
    all_to_all x1, blocking collectives, body(): lax.all_to_all(outgoing_rows, 'ep', split_axis=0, concat_axis=0, tiled=True)  177 us
    all_to_all x1, waiting for transfers between devices, body(): lax.all_to_all(produced.astype(jnp.bfloat16), 'ep', split_axis=0, concat_...  165 us
    all_to_all x1, blocking collectives, body(): lax.all_to_all(out_proj, 'ep', split_axis=1, concat_axis=0, tiled=True)  62.4 us
    all_gather x1, waiting for transfers between devices, body(): lax.all_gather(values, 'ep', axis=1, tiled=True)  61.1 us
    all_to_all x1, blocking collectives, body(): lax.all_to_all(outgoing, 'ep', split_axis=1, concat_axis=0, tiled=True)  61 us
    all_to_all x1, waiting for transfers between devices, body(): lax.all_to_all(column_share, 'ep', split_axis=0, concat_axis=1, tiled=True)  14.2 us
    all_to_all x1, starting transfers between devices, body(): lax.all_to_all(column_share, 'ep', split_axis=0, concat_axis=1, tiled=True)  14.2 us
  transfers between devices with their start and end apart: 3, of which 3 were waited for; matrix products, arithmetic and copies ran while one was open for 2% of the time, Pallas kernels for 0%

commit v1 on v0

--- a/solution.py
+++ b/solution.py
@@ -99,7 +99,17 @@
     values = values.astype(jnp.bfloat16).reshape(devices * tok_count, value_cols)
     turned = lax.all_to_all(out_proj, "ep", split_axis=1, concat_axis=0, tiled=True)
     column_share = jnp.dot(
-        lax.all_gather(values, "ep", axis=1, tiled=True), turned, preferred_element_type=jnp.float32
+        jnp.concatenate(
+            lax.all_to_all(
+                jnp.stack([values] * lax.axis_size("ep"), 0),
+                concat_axis=0,
+                split_axis=0,
+                axis_name="ep",
+            ),
+            1,
+        ),
+        turned,
+        preferred_element_type=jnp.float32,
     )
     attended = lax.all_to_all(column_share, "ep", split_axis=0, concat_axis=1, tiled=True)
     hidden = resid.reshape(tok_count, D).astype(jnp.float32) + attended

time: 702 us -> 1010 us (1.44)
  waiting for transfers between devices: 241 us -> 610 us
  blocking collectives: 300 us -> 177 us
  starting transfers between devices: 25.1 us -> 73.7 us
  local copies, waits for them, and re-layouts: 73.9 us -> 103 us
  between operations: 14 us -> 0.62 us
    all_to_all x0 -> x3, waiting for transfers between devices: none -> 430 us  [the longest x1 357 us: body(): lax.all_to_all(jnp.stack([values] * lax.axis_size('ep'), 0), concat_axis=...]
    all_to_all x2 -> x0, blocking collectives: 123 us -> none  [the longest x1 62.4 us: body(): lax.all_to_all(out_proj, 'ep', split_axis=1, concat_axis=0, tiled=True)]
    all_gather x1 -> x0, waiting for transfers between devices: 61.1 us -> none  [body(): lax.all_gather(values, 'ep', axis=1, tiled=True)]
    all_to_all x0 -> x3, starting transfers between devices: none -> 49.8 us  [the longest x1 29.4 us: body(): lax.all_to_all(outgoing, 'ep', split_axis=1, concat_axis=0, tiled=True)]
    reshape x0 -> x1, local copies, waits for them, and re-layouts: none -> 24 us  [body(): jnp.concatenate(lax.all_to_all(jnp.stack([values] * lax.axis_size('ep'),...]
    dot_general x2, local copies, waits for them, and re-layouts: 13.2 us -> 26 us  [body(): jnp.dot(jnp.concatenate(lax.all_to_all(jnp.stack([values] * lax.axis_size...]
    all_gather x1 -> x0, local copies, waits for them, and re-layouts: 11.4 us -> none  [body(): lax.all_gather(values, 'ep', axis=1, tiled=True)]
  transfers between devices with their start and end apart: 3 -> 5, of which waited for: 3 -> 5; matrix products, arithmetic and copies ran while one was open for 2% -> 2% of each run, Pallas kernels for 0% -> 0%
where the time goes in v1:
time: 1010 us; the launch traced here: 1000 us
  waiting for transfers between devices  610 us (60%)
  blocking collectives  177 us (18%)
  local copies, waits for them, and re-layouts  103 us (10%)
  starting transfers between devices  73.7 us (7%)
  matrix products  34 us (3%)
    all_to_all x1, waiting for transfers between devices, body(): lax.all_to_all(jnp.stack([values] * lax.axis_size('ep'), 0), concat_axis=...  357 us
    all_to_all x1, blocking collectives, body(): lax.all_to_all(outgoing_rows, 'ep', split_axis=0, concat_axis=0, tiled=True)  177 us
    all_to_all x1, waiting for transfers between devices, body(): lax.all_to_all(produced.astype(jnp.bfloat16), 'ep', split_axis=0, concat_...  165 us
    all_to_all x1, waiting for transfers between devices, body(): lax.all_to_all(out_proj, 'ep', split_axis=1, concat_axis=0, tiled=True)  46.7 us
    all_to_all x1, starting transfers between devices, body(): lax.all_to_all(outgoing, 'ep', split_axis=1, concat_axis=0, tiled=True)  29.4 us
    dot_general x2, local copies, waits for them, and re-layouts, body(): jnp.dot(jnp.concatenate(lax.all_to_all(jnp.stack([values] * lax.axis_size...  26 us
    all_to_all x1, waiting for transfers between devices, body(): lax.all_to_all(outgoing, 'ep', split_axis=1, concat_axis=0, tiled=True)  25.8 us
    reshape x1, local copies, waits for them, and re-layouts, body(): jnp.concatenate(lax.all_to_all(jnp.stack([values] * lax.axis_size('ep'),...  24 us
  transfers between devices with their start and end apart: 5, of which 5 were waited for; matrix products, arithmetic and copies ran while one was open for 2% of the time, Pallas kernels for 0%

profile of v1, /device:TPU:164, one launch (start us, length us, event | category | flops | bytes accessed | tf_op | source)
XLA Modules:
  0.0 1001.2 jit_solution(17122719681759785848)
XLA Ops:
  0.9 3.8 fusion.41
  5.5 1.7 fusion.5
  8.7 29.4 %all-to-all-start = ((bf16[4,128,512]{2,0,1:T(4,128)(2,1)}), bf16[4,128,512]{2,0,1:T(4,128)(2,1)S(1)}, u32[]{:S(2)}, u32[]{:S(2)}) async-start(bf16[4,128,512]{2,0,1:T(4,128)(2,1)} %bitcast.9), calls=%async_computation | async-start | bytes 1048576 | tf_op jit(solution)/shard_map/all_to_all | solution.py:96
  38.1 1.7 copy.54
  39.8 4.2 reshape.158
  44.1 25.8 %all-to-all-done = bf16[4,128,512]{2,0,1:T(4,128)(2,1)S(1)} async-done(((bf16[4,128,512]{2,0,1:T(4,128)(2,1)}), bf16[4,128,512]{2,0,1:T(4,128)(2,1)S(1)}, u32[]{:S(2)}, u32[]{:S(2)}) %all-to-all-start) | async-done | bytes 524320 | tf_op jit(solution)/shard_map/all_to_all | solution.py:96
  69.9 10.4 %all-to-all-start.2 = ((bf16[128,2,1792]{2,1,0:T(2,128)(2,1)}), bf16[128,2,1792]{2,1,0:T(2,128)(2,1)S(1)}, u32[]{:S(2)}, u32[]{:S(2)}) async-start(bf16[128,2,1792]{2,1,0:T(2,128)(2,1)} %reshape.158), calls=%async_computation.2 | async-start | bytes 1835008 | tf_op jit(solution)/shard_map/all_to_all | solution.py:100
  80.3 1.2 reshape.143
  81.8 46.7 %all-to-all-done.2 = bf16[128,2,1792]{2,1,0:T(2,128)(2,1)S(1)} async-done(((bf16[128,2,1792]{2,1,0:T(2,128)(2,1)}), bf16[128,2,1792]{2,1,0:T(2,128)(2,1)S(1)}, u32[]{:S(2)}, u32[]{:S(2)}) %all-to-all-start.2) | async-done | bytes 917536 | tf_op jit(solution)/shard_map/all_to_all | solution.py:100
  128.5 4.3 stack.3
  132.8 9.9 all-to-all-start.1
  142.7 2.0 reshape.159
  144.8 1.6 bitcast_bitcast_fusion
  146.4 1.8 copy.43
  148.2 3.0 reshape.154
  151.2 357.4 %all-to-all-done.1 = bf16[128,512,64]{1,2,0:T(8,128)(2,1)} async-done(((bf16[128,512,64]{1,2,0:T(8,128)(2,1)}), bf16[128,512,64]{1,2,0:T(8,128)(2,1)}, u32[]{:S(2)}, u32[]{:S(2)}) %all-to-all-start.1) | async-done | bytes 8388640 | tf_op jit(solution)/shard_map/all_to_all | solution.py:103
  508.5 24.0 %copy.41 = bf16[512,128,64]{2,1,0:T(8,128)(2,1)} copy(bf16[512,128,64]{0,2,1:T(8,128)(2,1)} %bitcast.12) | data formatting | bytes 16777216 | tf_op jit(solution)/shard_map/reshape | solution.py:102
  532.5 25.9 %dot_general.43 = bf16[128,4,8192]{2,1,0:T(4,128)(2,1)} reshape(bf16[512,128,64]{2,1,0:T(8,128)(2,1)} %copy.41) | data formatting | bytes 16777216 | tf_op jit(solution)/shard_map/dot_general | solution.py:101
  558.5 12.4 %fusion = f32[128,4,56]{0,2,1:T(8,128)S(1)} fusion(bf16[8192,56,1]{0,1,2:T(8,128)(2,1)S(1)} %reshape.154, bf16[128,4,8192]{2,1,0:T(4,128)(2,1)} %dot_general.43), kind=kOutput, calls=%fused_computation.2 | convolution fusion | flops 469762048 | bytes 9420800 | tf_op jit(solution)/shard_map/dot_general | solution.py:101
  571.9 13.0 %all-to-all-start.3 = ((f32[128,1,224]{2,1,0:T(1,128)}), f32[128,1,224]{2,1,0:T(1,128)S(1)}, u32[]{:S(2)}, u32[]{:S(2)}) async-start(f32[128,1,224]{2,1,0:T(1,128)} %reshape.160), calls=%async_computation.3 | async-start | bytes 262144 | tf_op jit(solution)/shard_map/all_to_all | solution.py:114
  585.5 14.2 %all-to-all-done.3 = f32[128,1,224]{2,1,0:T(1,128)S(1)} async-done(((f32[128,1,224]{2,1,0:T(1,128)}), f32[128,1,224]{2,1,0:T(1,128)S(1)}, u32[]{:S(2)}, u32[]{:S(2)}) %all-to-all-start.3) | async-done | bytes 114720 | tf_op jit(solution)/shard_map/all_to_all | solution.py:114
  603.1 1.2 convolution_convert_fusion.1
  604.2 3.8 copy.49
  608.0 176.9 %all_to_all.65 = bf16[128,2,7168]{2,1,0:T(2,128)(2,1)} all-to-all(bf16[128,2,7168]{2,1,0:T(2,128)(2,1)S(1)} %copy.49), channel_id=1, replica_groups=mesh['rep'=2,'ep'=128] {'ep'}, dimensions={0} | all-to-all | bytes 7340032 | tf_op jit(solution)/shard_map/all_to_all | solution.py:139
  784.9 8.4 reshape.145
  793.3 3.7 fusion.43
  797.1 6.6 convolution_convert_fusion
  803.6 8.1 convert_element_type.95
  811.8 10.9 %all-to-all-start.5 = ((bf16[128,2,7168]{2,1,0:T(2,128)(2,1)}), bf16[128,2,7168]{2,1,0:T(2,128)(2,1)}, u32[]{:S(2)}, u32[]{:S(2)}) async-start(bf16[128,2,7168]{2,1,0:T(2,128)(2,1)} %convert_element_type.95), calls=%async_computation.5 | async-start | bytes 7340032 | tf_op jit(solution)/shard_map/all_to_all | solution.py:143
  822.8 165.5 %all-to-all-done.5 = bf16[128,2,7168]{2,1,0:T(2,128)(2,1)} async-done(((bf16[128,2,7168]{2,1,0:T(2,128)(2,1)}), bf16[128,2,7168]{2,1,0:T(2,128)(2,1)}, u32[]{:S(2)}, u32[]{:S(2)}) %all-to-all-start.5) | async-done | bytes 3670048 | tf_op jit(solution)/shard_map/all_to_all | solution.py:143
  988.3 8.4 reshape.146
  996.7 3.6 fusion.2
  (63 shorter events, 9.0 us)
Async XLA Ops:
  0.0 797.0 %copy-start = (bf16[128,7168]{1,0:T(8,128)(2,1)S(1)}, bf16[128,7168]{1,0:T(8,128)(2,1)}, u32[]{:S(2)}) copy-start(bf16[128,7168]{1,0:T(8,128)(2,1)} %param.27) | copy-start | bytes 5505028
  0.9 3.8 copy-start.2
  0.9 3.8 copy-start.10
  0.9 4.6 copy-start.1
  7.2 30.9 %copy-start.4 = (bf16[64,7168]{1,0:T(8,128)(2,1)S(1)}, bf16[64,7168]{1,0:T(8,128)(2,1)}, u32[]{:S(2)}) copy-start(bf16[64,7168]{1,0:T(8,128)(2,1)} %param.20) | copy-start | bytes 2752516
  8.7 61.2 %all-to-all-start = ((bf16[4,128,512]{2,0,1:T(4,128)(2,1)}), bf16[4,128,512]{2,0,1:T(4,128)(2,1)S(1)}, u32[]{:S(2)}, u32[]{:S(2)}) async-start(bf16[4,128,512]{2,0,1:T(4,128)(2,1)} %bitcast.9), calls=%async_computation | async-start | bytes 1048576 | tf_op jit(solution)/shard_map/all_to_all | solution.py:96
  38.1 43.4 %copy-start.7 = (bf16[512,64]{0,1:T(8,128)(2,1)S(1)}, bf16[512,64]{0,1:T(8,128)(2,1)}, u32[]{:S(2)}) copy-start(bf16[512,64]{0,1:T(8,128)(2,1)} %param.19) | copy-start | bytes 196612
  69.9 10.4 %copy-start.3 = (bf16[4,128,512]{2,0,1:T(4,128)(2,1)}, bf16[4,128,512]{2,0,1:T(4,128)(2,1)S(1)}, u32[]{:S(2)}) copy-start(bf16[4,128,512]{2,0,1:T(4,128)(2,1)S(1)} %all-to-all-done) | copy-start | bytes 1572868
  69.9 58.6 %all-to-all-start.2 = ((bf16[128,2,1792]{2,1,0:T(2,128)(2,1)}), bf16[128,2,1792]{2,1,0:T(2,128)(2,1)S(1)}, u32[]{:S(2)}, u32[]{:S(2)}) async-start(bf16[128,2,1792]{2,1,0:T(2,128)(2,1)} %reshape.158), calls=%async_computation.2 | async-start | bytes 1835008 | tf_op jit(solution)/shard_map/all_to_all | solution.py:100
  132.8 375.7 %all-to-all-start.1 = ((bf16[128,512,64]{1,2,0:T(8,128)(2,1)}), bf16[128,512,64]{1,2,0:T(8,128)(2,1)}, u32[]{:S(2)}, u32[]{:S(2)}) async-start(bf16[128,512,64]{1,2,0:T(8,128)(2,1)} %stack.3), calls=%async_computation.1 | async-start | bytes 16777216 | tf_op jit(solution)/shard_map/all_to_all | solution.py:103
  558.4 26.6 %copy-start.6 = (bf16[2,2,7168]{2,1,0:T(2,128)(2,1)S(1)}, bf16[2,2,7168]{2,1,0:T(2,128)(2,1)}, u32[]{:S(2)}) copy-start(bf16[2,2,7168]{2,1,0:T(2,128)(2,1)} %param.18) | copy-start | bytes 172036
  558.4 26.8 %copy-start.8 = (bf16[7168]{0:T(1024)(128)(2,1)S(1)}, bf16[7168]{0:T(1024)(128)(2,1)}, u32[]{:S(2)}) copy-start(bf16[7168]{0:T(1024)(128)(2,1)} %param.21) | copy-start | bytes 43012
  558.4 26.9 %copy-start.11 = (s32[2,2,8]{2,1,0:T(2,128)S(1)}, s32[2,2,8]{2,1,0:T(2,128)}, u32[]{:S(2)}) copy-start(s32[2,2,8]{2,1,0:T(2,128)} %param.24) | copy-start | bytes 388
  558.5 27.0 %copy-start.9 = (s32[2,2,8]{2,1,0:T(2,128)S(1)}, s32[2,2,8]{2,1,0:T(2,128)}, u32[]{:S(2)}) copy-start(s32[2,2,8]{2,1,0:T(2,128)} %param.23) | copy-start | bytes 388
  570.8 31.0 %copy-start.5 = (bf16[7168,16]{0,1:T(8,128)(2,1)S(1)}, bf16[7168,16]{0,1:T(8,128)(2,1)}, u32[]{:S(2)}) copy-start(bf16[7168,16]{0,1:T(8,128)(2,1)} %param.22) | copy-start | bytes 688132
  571.9 27.8 %all-to-all-start.3 = ((f32[128,1,224]{2,1,0:T(1,128)}), f32[128,1,224]{2,1,0:T(1,128)S(1)}, u32[]{:S(2)}, u32[]{:S(2)}) async-start(f32[128,1,224]{2,1,0:T(1,128)} %reshape.160), calls=%async_computation.3 | async-start | bytes 262144 | tf_op jit(solution)/shard_map/all_to_all | solution.py:114
  811.8 176.5 %all-to-all-start.5 = ((bf16[128,2,7168]{2,1,0:T(2,128)(2,1)}), bf16[128,2,7168]{2,1,0:T(2,128)(2,1)}, u32[]{:S(2)}, u32[]{:S(2)}) async-start(bf16[128,2,7168]{2,1,0:T(2,128)(2,1)} %convert_element_type.95), calls=%async_computation.5 | async-start | bytes 7340032 | tf_op jit(solution)/shard_map/all_to_all | solution.py:143
